TPU v7x, 32 devices: a whole 2x2x4 slice. The times are simulated.
32 devices in a mesh: dp: 8 (over z, y), mp: 4 (over x, core).
Axes of the slice: x: 2, y: 2, z: 4, core: 2. Of those that a mesh axis runs over, the one named last changes fastest.
Arguments:
- image_tokens: bfloat16 [8, 192, 3072], P('dp'), may hold values from -6 to 6
- text_tokens: bfloat16 [8, 64, 3072], P('dp'), may hold values from -6 to 6
- null_prompt: bfloat16 [64, 3072], replicated, may hold values from -6 to 6
- drop_flags: int32 [8], P('dp'), may hold values 0 or 1
- time_index: int32 [8], P('dp'), may hold values from 0 to 31
- modulation: float32 [32, 3, 3072], replicated, may hold values from -3 to 3
- w_up: bfloat16 [3072, 12288], P('dp', 'mp'), may hold values from -0.109375 to 0.109375
- w_down: bfloat16 [12288, 3072], P('mp', 'dp'), may hold values from -0.0546875 to 0.0546875
- d_output: bfloat16 [8, 256, 3072], P('dp'), may hold values from -6 to 6
Outputs:
- block_out: bfloat16 [8, 256, 3072], P('dp')
- d_tokens: bfloat16 [8, 256, 3072], P('dp')
- grad_up: float32 [3072, 12288], P('dp', 'mp')
- grad_down: float32 [12288, 3072], P('mp', 'dp')
- grad_null: float32 [64, 3072], replicated
All inputs are finite; a program needn't handle non-finite values. No bound on the sum of `drop_flags` on one device may be relied on, other than what follows from the above.
Results may differ from a plain program's by a relative error of at most 0.017.
Values may be sent and summed in bfloat16 or wider, within the bound.
A program may use at most 128 MiB of HBM per device.

v0:
```python
import jax
import jax.numpy as jnp
from jax import lax
from jax.sharding import PartitionSpec as P

EPS = 1e-06


def gelu_tanh(values):
    return jax.nn.gelu(values, approximate=True)


def contract_rows(left, right):
    return lax.dot_general(
        left, right, (((0,), (0,)), ((), ())), preferred_element_type=jnp.float32
    )


def contract_cols(left, right):
    return lax.dot_general(
        left, right, (((1,), (1,)), ((), ())), preferred_element_type=jnp.float32
    )


def shards(
    image_tokens,
    text_tokens,
    null_prompt,
    drop_flags,
    time_index,
    modulation,
    w_up,
    w_down,
    d_output,
):
    dropped = drop_flags == 1
    text_in = jnp.where(dropped[:, None, None], null_prompt[None], text_tokens)
    joined = jnp.concatenate([text_in, image_tokens], axis=1)
    levels = jnp.arange(modulation.shape[0], dtype=jnp.int32)
    indicator_matrix = (time_index[:, None] == levels[None, :]).astype(jnp.float32)
    modulation_vectors = jnp.einsum(
        "yi,imr->ymr", indicator_matrix, modulation, precision=lax.Precision.HIGHEST
    )
    shift_modulation = modulation_vectors[:, 0][:, None]
    scale_mod = modulation_vectors[:, 1][:, None]
    gate_mod = modulation_vectors[:, 2][:, None]
    batch, length, width = joined.shape
    joined32 = joined.astype(jnp.float32)
    centred = joined32 - jnp.mean(joined32, axis=-1, keepdims=True)
    inv_std = lax.rsqrt(jnp.mean(centred * centred, axis=-1, keepdims=True) + EPS)
    normed = centred * inv_std
    mod_in = (normed * (1.0 + scale_mod) + shift_modulation).astype(jnp.bfloat16)
    flat_in = mod_in.reshape(batch * length, width)
    full_up, full_down = (
        lax.all_gather(w_up, "dp", axis=0, tiled=True),
        lax.all_gather(w_down, "dp", axis=1, tiled=True),
    )
    preactivation_rows = jnp.dot(flat_in, full_up, preferred_element_type=jnp.float32)
    hidden = gelu_tanh(preactivation_rows).astype(jnp.bfloat16)
    partial_value = jnp.dot(hidden, full_down, preferred_element_type=jnp.float32)
    branch = (
        lax.psum(partial_value.astype(jnp.bfloat16), "mp")
        .astype(jnp.float32)
        .reshape(batch, length, width)
    )
    block_out = (joined32 + gate_mod * branch).astype(jnp.bfloat16)
    d_out32 = d_output.astype(jnp.float32)
    d_branch = (d_out32 * gate_mod).astype(jnp.bfloat16).reshape(batch * length, width)
    hidden_gradient = contract_cols(d_branch, full_down)
    _, gelu_back = jax.vjp(gelu_tanh, preactivation_rows)
    d_pre = gelu_back(hidden_gradient)[0].astype(jnp.bfloat16)
    d_part = contract_cols(d_pre, full_up)
    d_mod = lax.psum(d_part.astype(jnp.bfloat16), "mp").astype(jnp.float32)
    owned_mod, owned_branch = (
        lax.all_to_all(flat_in, "dp", split_axis=1, concat_axis=0, tiled=True),
        lax.all_to_all(d_branch, "dp", split_axis=1, concat_axis=0, tiled=True),
    )
    grad_up = contract_rows(owned_mod, lax.all_gather(d_pre, "dp", axis=0, tiled=True))
    grad_down_t = contract_rows(owned_branch, lax.all_gather(hidden, "dp", axis=0, tiled=True))
    grad_down = grad_down_t.T
    d_normed = d_mod.reshape(batch, length, width) * (1.0 + scale_mod)
    d_full = d_out32 + inv_std * (
        d_normed
        - jnp.mean(d_normed, axis=-1, keepdims=True)
        - normed * jnp.mean(d_normed * normed, axis=-1, keepdims=True)
    )
    text_len = null_prompt.shape[0]
    null_part = jnp.sum(
        jnp.where(dropped[:, None, None], d_full[:, :text_len], jnp.float32(0.0)), axis=0
    )
    grad_null = lax.psum(null_part.astype(jnp.bfloat16), "dp").astype(jnp.float32)
    return (block_out, d_full.astype(jnp.bfloat16), grad_up, grad_down, grad_null)


def solution(mesh):
    placed = (
        P("dp", None, None),
        P("dp", None, None),
        P(),
        P("dp"),
        P("dp"),
        P(),
        P("dp", "mp"),
        P("mp", "dp"),
        P("dp", None, None),
    )
    return jax.shard_map(
        shards,
        mesh=mesh,
        in_specs=placed,
        out_specs=(P("dp", None, None), P("dp", None, None), P("dp", "mp"), P("mp", "dp"), P()),
        check_vma=False,
    )
```

profile of v0, /device:TPU:0, one launch (start us, length us, event | category | flops | bytes accessed | tf_op | source)
XLA Modules:
  0.0 1318.2 jit_solution(9674357997162976993)
XLA Ops:
  7.2 0.0 copy-start
  7.2 0.0 copy-start.8
  7.2 0.0 all-gather.5.cloned.1.call-start
  7.3 0.7 all-gather.5.cloned.1.call-update
  7.9 0.0 all-gather.7.cloned.1.call-start
  8.0 0.7 all-gather.7.cloned.1.call-update
  8.7 0.0 all-reduce.6.cloned.1.call-start
  8.7 0.0 copy-start.4
  10.2 0.3 convert_reduce_fusion
  10.5 0.6 fusion.12
  11.1 0.5 fusion.36
  11.6 0.1 fusion.41
  11.7 1.5 fusion.13
  13.2 361.5 %all-gather.5.cloned.1.call-done = bf16[3072,3072]{1,0:T(8,128)(2,1)} async-done(((bf16[384,3072]{1,0:T(8,128)(2,1)}), bf16[3072,3072]{1,0:T(8,128)(2,1)}) %all-gather.5.cloned.1.call-update) | async-done | bytes 18874384 | tf_op jit(solution)/shard_map/all_gather | solution.py:55
  374.7 14.2 %multiply_convert_fusion = (bf16[256,3072]{1,0:T(8,128)(2,1)}, f32[256,3072]{1,0:T(8,128)}) fusion(bf16[3072,3072]{1,0:T(8,128)(2,1)} %all-gather.5.cloned.1.call-done, f32[3072]{0:T(1024)S(1)} %bitcast.82, f32[3072]{0:T(1024)S(1)} %bitcast.79, f32[256]{0:T(256)S(1)} %add_rsqrt_fusion, f32[256]{0:T(256)S(1)} %broadcast_multiply_fusion.2, ...), kind=kOutput, calls=%fused_computation.34 | convolution fusion | flops 4845993984 | bytes 25192448 | tf_op jit(solution)/shard_map/dot_general | solution.py:58
  388.9 349.8 %all-gather.7.cloned.1.call-done = bf16[3072,3072]{1,0:T(8,128)(2,1)} async-done(((bf16[3072,384]{1,0:T(8,128)(2,1)}), bf16[3072,3072]{1,0:T(8,128)(2,1)}) %all-gather.7.cloned.1.call-update) | async-done | bytes 18874384 | tf_op jit(solution)/shard_map/all_gather | solution.py:56
  738.7 12.3 fusion.20
  751.0 10.3 convolution_convert_fusion
  761.3 10.3 convolution_convert_fusion.1
  771.6 0.0 all-reduce.6.cloned.1.call-update
  771.6 0.0 all-reduce.4.cloned.1.call-start
  771.7 68.5 %all-reduce.6.cloned.1.call-done = (bf16[256,3072]{1,0:T(8,128)(2,1)}, bf16[256,3072]{1,0:T(8,128)(2,1)}) async-done(((bf16[256,3072]{1,0:T(8,128)(2,1)}, bf16[256,3072]{1,0:T(8,128)(2,1)}), (bf16[256,3072]{1,0:T(8,128)(2,1)}, bf16[256,3072]{1,0:T(8,128)(2,1)})) %all-reduce.6.cloned.1.call-update) | async-done | bytes 3145744 | tf_op jit(solution)/shard_map/psum | solution.py:62
  840.2 4.4 fusion.21
  844.6 1.6 convert_add_fusion
  846.3 0.0 copy-start.7
  846.3 1.1 copy-done.7
  847.4 0.8 fusion.34
  848.2 0.0 all-reduce.4.cloned.1.call-update
  848.2 0.0 all-gather.9.cloned.1.call-start
  848.3 0.5 all-gather.9.cloned.1.call-update
  848.8 0.0 all-gather.11.cloned.1.call-start
  848.9 0.5 all-gather.11.cloned.1.call-update
  849.5 0.2 copy.25
  849.7 2.5 add_convert_fusion
  852.3 0.0 copy-start.3
  852.3 1.3 copy.18
  853.6 5.5 all-to-all-start
  859.1 0.3 copy.26
  859.4 1.4 copy.19
  860.8 37.9 %all-to-all-done = bf16[256,8,384]{2,0,1:T(8,128)(2,1)} async-done(((bf16[256,8,384]{2,0,1:T(8,128)(2,1)}), bf16[256,8,384]{2,0,1:T(8,128)(2,1)}, u32[]{:S(2)}, u32[]{:S(2)}) %all-to-all-start) | async-done | bytes 1572896 | tf_op jit(solution)/shard_map/all_to_all | solution.py:75
  898.7 3.8 all-to-all-start.1
  902.4 44.3 %all-reduce.4.cloned.1.call-done = bf16[64,3072]{1,0:T(8,128)(2,1)} async-done(((bf16[64,3072]{1,0:T(8,128)(2,1)}), bf16[64,3072]{1,0:T(8,128)(2,1)}) %all-reduce.4.cloned.1.call-update) | async-done | bytes 393232 | tf_op jit(solution)/shard_map/psum | solution.py:91
  946.7 1.9 convert_element_type.92
  948.7 175.1 %all-gather.9.cloned.1.call-done = bf16[2048,3072]{1,0:T(8,128)(2,1)} async-done(((bf16[256,3072]{1,0:T(8,128)(2,1)}), bf16[2048,3072]{1,0:T(8,128)(2,1)}) %all-gather.9.cloned.1.call-update) | async-done | bytes 12582928 | tf_op jit(solution)/shard_map/all_gather | solution.py:78
  1123.7 9.9 fusion.43
  1133.7 0.0 all-to-all-done.1
  1133.7 166.4 %all-gather.11.cloned.1.call-done = bf16[2048,3072]{1,0:T(8,128)(2,1)} async-done(((bf16[256,3072]{1,0:T(8,128)(2,1)}), bf16[2048,3072]{1,0:T(8,128)(2,1)}) %all-gather.11.cloned.1.call-update) | async-done | bytes 12582928 | tf_op jit(solution)/shard_map/all_gather | solution.py:79
  1300.1 11.2 fusion.44
  (22 shorter events, 0.2 us)
Async XLA Ops:
  7.2 4.0 copy-start
  7.2 3.0 copy-start.8
  7.2 3.0 copy-start.9
  7.2 3.0 copy-start.2
  7.2 367.5 %all-gather.5.cloned.1.call-start = ((), (), s32[]{:S(2)}) async-start(), calls=%async_computation.2 | async-start | bytes 21233664 | tf_op jit(solution)/shard_map/all_gather | solution.py:55
  7.9 730.7 %all-gather.7.cloned.1.call-start = ((), (), s32[]{:S(2)}) async-start(), calls=%async_computation.3 | async-start | bytes 21233664 | tf_op jit(solution)/shard_map/all_gather | solution.py:56
  8.7 831.5 %all-reduce.6.cloned.1.call-start = ((), (), s32[]{:S(2)}) async-start(), calls=%async_computation.7 | async-start | bytes 6291456 | tf_op jit(solution)/shard_map/psum | solution.py:62
  8.7 3.0 copy-start.4
  771.6 175.1 %all-reduce.4.cloned.1.call-start = ((), (), s32[]{:S(2)}) async-start(), calls=%async_computation.6 | async-start | bytes 786432 | tf_op jit(solution)/shard_map/psum | solution.py:91
  840.2 4.4 copy-start.5
  840.2 4.4 copy-start.6
  846.3 1.1 copy-start.7
  848.2 275.5 %all-gather.9.cloned.1.call-start = ((), (), s32[]{:S(2)}) async-start(), calls=%async_computation.4 | async-start | bytes 14155776 | tf_op jit(solution)/shard_map/all_gather | solution.py:78
  848.8 451.3 %all-gather.11.cloned.1.call-start = ((), (), s32[]{:S(2)}) async-start(), calls=%async_computation.5 | async-start | bytes 14155776 | tf_op jit(solution)/shard_map/all_gather | solution.py:79
  852.3 6.9 copy-start.3
  853.6 45.0 %all-to-all-start = ((bf16[256,8,384]{2,0,1:T(8,128)(2,1)}), bf16[256,8,384]{2,0,1:T(8,128)(2,1)}, u32[]{:S(2)}, u32[]{:S(2)}) async-start(bf16[256,8,384]{2,0,1:T(8,128)(2,1)} %copy.18), calls=%async_computation | async-start | bytes 3145728 | tf_op jit(solution)/shard_map/all_to_all | solution.py:75
  898.7 235.0 %all-to-all-start.1 = ((bf16[256,8,384]{2,0,1:T(8,128)(2,1)}), bf16[256,8,384]{2,0,1:T(8,128)(2,1)S(1)}, u32[]{:S(2)}, u32[]{:S(2)}) async-start(bf16[256,8,384]{2,0,1:T(8,128)(2,1)} %copy.19), calls=%async_computation.1 | async-start | bytes 3145728 | tf_op jit(solution)/shard_map/all_to_all | solution.py:76
  1300.1 11.2 copy-start.1
Sparse Core Ops, SparseCore 0:
  9.6 365.1 all-gather.4
  376.3 362.3 all-gather.6
  771.7 68.4 all-reduce.5
  848.4 98.3 all-reduce.3
  948.8 174.9 all-gather.8
  1125.8 174.2 all-gather.10
where the time goes:
time: 1320 us
  waiting for transfers between devices  1210 us (92%)
  matrix products  68.8 us (5%)
  between operations  15.7 us (1%)
  other arithmetic  13.8 us (1%)
    all_gather x1, waiting for transfers between devices, shards(): lax.all_gather(w_up, 'dp', axis=0, tiled=True)  362 us
    all_gather x1, waiting for transfers between devices, shards(): lax.all_gather(w_down, 'dp', axis=1, tiled=True)  350 us
    all_gather x1, waiting for transfers between devices, shards(): lax.all_gather(d_pre, 'dp', axis=0, tiled=True)  175 us
    all_gather x1, waiting for transfers between devices, shards(): lax.all_gather(hidden, 'dp', axis=0, tiled=True)  166 us
    psum x1, waiting for transfers between devices, shards(): lax.psum(partial_value.astype(jnp.bfloat16), 'mp').astype(jnp.float32)  68.5 us
    psum x1, waiting for transfers between devices, shards(): lax.psum(null_part.astype(jnp.bfloat16), 'dp').astype(jnp.float32)  44.3 us
    all_to_all x1, waiting for transfers between devices, shards(): lax.all_to_all(flat_in, 'dp', split_axis=1, concat_axis=0, tiled=True)  37.9 us
  transfers between devices with their start and end apart: 8, of which 7 were waited for; matrix products, arithmetic and copies ran while one was open for 3% of the time, Pallas kernels for 0%

commit v1 on v0

--- a/solution.py
+++ b/solution.py
@@ -4,6 +4,12 @@
 from jax.sharding import PartitionSpec as P
 
 EPS = 1e-06
+
+
+def gather_and_add(value, mesh_axis):
+    parts = lax.all_gather(value, mesh_axis, axis=0, tiled=False)
+    summed = parts.sum(axis=0)
+    return summed
 
 
 def gelu_tanh(values):
@@ -59,7 +65,7 @@
     hidden = gelu_tanh(preactivation_rows).astype(jnp.bfloat16)
     partial_value = jnp.dot(hidden, full_down, preferred_element_type=jnp.float32)
     branch = (
-        lax.psum(partial_value.astype(jnp.bfloat16), "mp")
+        gather_and_add(partial_value.astype(jnp.bfloat16), "mp")
         .astype(jnp.float32)
         .reshape(batch, length, width)
     )

time: 1320 us -> 1350 us (1.023)
    all_gather x0 -> x1, waiting for transfers between devices: none -> 46.2 us  [gather_and_add(): parts = lax.all_gather(value, mesh_axis, axis=0, tiled=False)]
    all_to_all x1, waiting for transfers between devices: 37.9 us -> 0.01 us  [shards(): lax.all_to_all(flat_in, 'dp', split_axis=1, concat_axis=0, tiled=True)]
    all_to_all x1, waiting for transfers between devices: 0.01 us -> 34.8 us  [shards(): lax.all_to_all(d_branch, 'dp', split_axis=1, concat_axis=0, tiled=True)]
    psum x1, waiting for transfers between devices: 68.5 us -> 43 us  [shards(): d_mod = lax.psum(d_part.astype(jnp.bfloat16), 'mp').astype(jnp.float32)]
  transfers between devices with their start and end apart: 8 -> 9, of which waited for: 7 -> 8; matrix products, arithmetic and copies ran while one was open for 3% -> 3% of each run, Pallas kernels for 0% -> 0%
where the time goes in v1:
time: 1350 us
  waiting for transfers between devices  1220 us (90%)
  matrix products  68.8 us (5%)
  other arithmetic  21.5 us (2%)
  between operations  15.6 us (1%)
    all_gather x1, waiting for transfers between devices, shards(): lax.all_gather(w_up, 'dp', axis=0, tiled=True)  363 us
    all_gather x1, waiting for transfers between devices, shards(): lax.all_gather(w_down, 'dp', axis=1, tiled=True)  350 us
    all_gather x1, waiting for transfers between devices, shards(): lax.all_gather(hidden, 'dp', axis=0, tiled=True)  176 us
    all_gather x1, waiting for transfers between devices, shards(): lax.all_gather(d_pre, 'dp', axis=0, tiled=True)  165 us
    all_gather x1, waiting for transfers between devices, gather_and_add(): parts = lax.all_gather(value, mesh_axis, axis=0, tiled=False)  46.2 us
    psum x1, waiting for transfers between devices, shards(): lax.psum(null_part.astype(jnp.bfloat16), 'dp').astype(jnp.float32)  43.7 us
    psum x1, waiting for transfers between devices, shards(): d_mod = lax.psum(d_part.astype(jnp.bfloat16), 'mp').astype(jnp.float32)  43 us
    all_to_all x1, waiting for transfers between devices, shards(): lax.all_to_all(d_branch, 'dp', split_axis=1, concat_axis=0, tiled=True)  34.8 us
  transfers between devices with their start and end apart: 9, of which 8 were waited for; matrix products, arithmetic and copies ran while one was open for 3% of the time, Pallas kernels for 0%

profile of v1, /device:TPU:0, one launch (start us, length us, event | category | flops | bytes accessed | tf_op | source)
XLA Modules:
  0.0 1347.7 jit_solution(9799871473807547904)
XLA Ops:
  7.2 0.0 copy-start
  7.2 0.0 all-gather.7.cloned.1.call-start
  7.3 0.7 all-gather.7.cloned.1.call-update
  7.9 0.0 all-gather.9.cloned.1.call-start
  8.0 0.7 all-gather.9.cloned.1.call-update
  8.7 0.0 all-gather.15.cloned.1.call-start
  10.1 0.3 convert_reduce_fusion
  10.4 0.6 fusion.9
  11.0 0.5 fusion.24
  11.5 0.1 fusion.30
  11.6 363.1 %all-gather.7.cloned.1.call-done = bf16[3072,3072]{1,0:T(8,128)(2,1)} async-done(((bf16[384,3072]{1,0:T(8,128)(2,1)}), bf16[3072,3072]{1,0:T(8,128)(2,1)}) %all-gather.7.cloned.1.call-update) | async-done | bytes 18874384 | tf_op jit(solution)/shard_map/all_gather | solution.py:61
  374.7 14.2 %multiply_convert_fusion = (bf16[256,3072]{1,0:T(8,128)(2,1)}, f32[256,3072]{1,0:T(8,128)}) fusion(bf16[3072,3072]{1,0:T(8,128)(2,1)} %all-gather.7.cloned.1.call-done, f32[3072]{0:T(1024)S(1)} %bitcast.82, f32[3072]{0:T(1024)S(1)} %bitcast.78, f32[256]{0:T(256)S(1)} %add_rsqrt_fusion, f32[256]{0:T(256)S(1)} %broadcast_multiply_fusion.2, ...), kind=kOutput, calls=%fused_computation.25 | convolution fusion | flops 4845993984 | bytes 25192448 | tf_op jit(solution)/shard_map/dot_general | solution.py:64
  388.9 349.8 %all-gather.9.cloned.1.call-done = bf16[3072,3072]{1,0:T(8,128)(2,1)} async-done(((bf16[3072,384]{1,0:T(8,128)(2,1)}), bf16[3072,3072]{1,0:T(8,128)(2,1)}) %all-gather.9.cloned.1.call-update) | async-done | bytes 18874384 | tf_op jit(solution)/shard_map/all_gather | solution.py:62
  738.7 10.3 convolution_convert_fusion.1
  749.0 0.0 all-gather.15.cloned.1.call-update
  749.0 0.2 all-reduce.3.cloned.1.call-start
  749.2 46.2 %all-gather.15.cloned.1.call-done = bf16[1024,3072]{1,0:T(8,128)(2,1)} async-done(((bf16[256,3072]{1,0:T(8,128)(2,1)}), bf16[1024,3072]{1,0:T(8,128)(2,1)}) %all-gather.15.cloned.1.call-update) | async-done | bytes 6291472 | tf_op jit(solution)/shard_map/all_gather | solution.py:10
  795.5 5.5 reduce_sum.54
  801.0 4.0 fusion
  805.0 1.2 copy-done.3
  806.1 11.6 fusion.7
  817.7 10.3 convolution_convert_fusion
  828.0 0.0 all-reduce.3.cloned.1.call-update
  828.0 0.0 all-reduce.5.cloned.1.call-start
  828.1 43.0 %all-reduce.3.cloned.1.call-done = bf16[256,3072]{1,0:T(8,128)(2,1)} async-done(((bf16[256,3072]{1,0:T(8,128)(2,1)}), bf16[256,3072]{1,0:T(8,128)(2,1)}) %all-reduce.3.cloned.1.call-update) | async-done | bytes 1572880 | tf_op jit(solution)/shard_map/psum | solution.py:79
  871.0 2.5 fusion.11
  873.5 3.0 convert_add_fusion.1
  876.6 1.1 copy-done.5
  877.7 0.8 fusion.22
  878.5 0.0 all-reduce.5.cloned.1.call-update
  878.5 0.0 all-gather.13.cloned.1.call-start
  878.6 0.5 all-gather.13.cloned.1.call-update
  879.1 0.0 all-gather.11.cloned.1.call-start
  879.2 0.7 all-gather.11.cloned.1.call-update
  879.9 1.7 copy.26
  881.6 1.3 copy.19
  882.9 5.5 all-to-all-start.1
  888.4 1.2 copy.25
  889.7 2.7 add_convert_fusion
  892.5 1.3 copy.18
  893.8 34.8 %all-to-all-done.1 = bf16[256,8,384]{2,0,1:T(8,128)(2,1)} async-done(((bf16[256,8,384]{2,0,1:T(8,128)(2,1)}), bf16[256,8,384]{2,0,1:T(8,128)(2,1)}, u32[]{:S(2)}, u32[]{:S(2)}) %all-to-all-start.1) | async-done | bytes 1572896 | tf_op jit(solution)/shard_map/all_to_all | solution.py:82
  928.6 3.8 all-to-all-start
  932.4 43.7 %all-reduce.5.cloned.1.call-done = bf16[64,3072]{1,0:T(8,128)(2,1)} async-done(((bf16[64,3072]{1,0:T(8,128)(2,1)}), bf16[64,3072]{1,0:T(8,128)(2,1)}) %all-reduce.5.cloned.1.call-update) | async-done | bytes 393232 | tf_op jit(solution)/shard_map/psum | solution.py:97
  976.0 1.9 convert_element_type.113
  978.0 176.0 %all-gather.13.cloned.1.call-done = bf16[2048,3072]{1,0:T(8,128)(2,1)} async-done(((bf16[256,3072]{1,0:T(8,128)(2,1)}), bf16[2048,3072]{1,0:T(8,128)(2,1)}) %all-gather.13.cloned.1.call-update) | async-done | bytes 12582928 | tf_op jit(solution)/shard_map/all_gather | solution.py:85
  1153.9 11.6 fusion.33
  1165.5 164.9 %all-gather.11.cloned.1.call-done = bf16[2048,3072]{1,0:T(8,128)(2,1)} async-done(((bf16[256,3072]{1,0:T(8,128)(2,1)}), bf16[2048,3072]{1,0:T(8,128)(2,1)}) %all-gather.11.cloned.1.call-update) | async-done | bytes 12582928 | tf_op jit(solution)/shard_map/all_gather | solution.py:84
  1330.4 10.4 fusion.32
  (24 shorter events, 0.2 us)
Async XLA Ops:
  7.2 3.8 copy-start
  7.2 2.9 copy-start.6
  7.2 2.9 copy-start.7
  7.2 2.9 copy-start.2
  7.2 367.5 %all-gather.7.cloned.1.call-start = ((), (), s32[]{:S(2)}) async-start(), calls=%async_computation.2 | async-start | bytes 21233664 | tf_op jit(solution)/shard_map/all_gather | solution.py:61
  7.9 730.7 %all-gather.9.cloned.1.call-start = ((), (), s32[]{:S(2)}) async-start(), calls=%async_computation.3 | async-start | bytes 21233664 | tf_op jit(solution)/shard_map/all_gather | solution.py:62
  8.7 786.8 %all-gather.15.cloned.1.call-start = ((), (), s32[]{:S(2)}) async-start(), calls=%async_computation.8 | async-start | bytes 7864320 | tf_op jit(solution)/shard_map/all_gather | solution.py:10
  749.0 122.1 %all-reduce.3.cloned.1.call-start = ((), (), s32[]{:S(2)}) async-start(), calls=%async_computation.4 | async-start | bytes 3145728 | tf_op jit(solution)/shard_map/psum | solution.py:79
  801.0 5.2 copy-start.8
  805.0 1.2 copy-start.3
  828.0 148.0 %all-reduce.5.cloned.1.call-start = ((), (), s32[]{:S(2)}) async-start(), calls=%async_computation.7 | async-start | bytes 786432 | tf_op jit(solution)/shard_map/psum | solution.py:97
  871.0 2.5 copy-start.4
  876.6 1.1 copy-start.5
  878.5 275.4 %all-gather.13.cloned.1.call-start = ((), (), s32[]{:S(2)}) async-start(), calls=%async_computation.6 | async-start | bytes 14155776 | tf_op jit(solution)/shard_map/all_gather | solution.py:85
  879.1 451.3 %all-gather.11.cloned.1.call-start = ((), (), s32[]{:S(2)}) async-start(), calls=%async_computation.5 | async-start | bytes 14155776 | tf_op jit(solution)/shard_map/all_gather | solution.py:84
  882.9 45.7 %all-to-all-start.1 = ((bf16[256,8,384]{2,0,1:T(8,128)(2,1)}), bf16[256,8,384]{2,0,1:T(8,128)(2,1)}, u32[]{:S(2)}, u32[]{:S(2)}) async-start(bf16[256,8,384]{2,0,1:T(8,128)(2,1)} %copy.19), calls=%async_computation.1 | async-start | bytes 3145728 | tf_op jit(solution)/shard_map/all_to_all | solution.py:82
  928.6 236.9 %all-to-all-start = ((bf16[256,8,384]{2,0,1:T(8,128)(2,1)}), bf16[256,8,384]{2,0,1:T(8,128)(2,1)S(1)}, u32[]{:S(2)}, u32[]{:S(2)}) async-start(bf16[256,8,384]{2,0,1:T(8,128)(2,1)} %copy.18), calls=%async_computation | async-start | bytes 3145728 | tf_op jit(solution)/shard_map/all_to_all | solution.py:81
  1330.4 10.4 copy-start.1
Sparse Core Ops, SparseCore 0:
  9.6 365.1 all-gather.6
  376.3 362.3 all-gather.8
  749.1 46.3 all-gather.14
  828.1 42.8 all-reduce.2
  878.7 97.3 all-reduce.4
  978.7 175.2 all-gather.12
  1156.1 174.2 all-gather.10
